TPU v7x, 32 devices: a whole 2x2x4 slice. The times are simulated.
32 devices in a mesh: grp: 2 (over y), kv: 8 (over z, core), hd: 2 (over x), sub: 1.
Axes of the slice: x: 2, y: 2, z: 4, core: 2. Of those that a mesh axis runs over, the one named last changes fastest.
Arguments:
- queries: bfloat16 [256, 8192], P(('grp', 'kv'), 'hd'), parts along dimension 0, may hold values from -12 to 12
- prompt_of: int32 [256, 1], P('grp'), parts along dimension 0, may hold values from 0 to 1; in each aligned block of 16 rows (0 to 15, 16 to 31, ...) at most 8 rows name the same one
- prompt_len: int32 [4], P('grp'), parts along dimension 0, may hold values from 3072 to 4096
- suffix_len: int32 [256], P(('grp', 'kv')), parts along dimension 0, may hold values from 0 to 512
- page_table: int32 [256, 8], P(('grp', 'kv'), 'sub'), parts along dimension 0, may hold values from 0 to 127, as said below
- prompt_keys: bfloat16 [16384, 1024], P(('grp', 'kv', 'sub'), 'hd'), parts along dimension 0, may hold values from -14 to 14
- shared_prompt_values: bfloat16 [16384, 1024], P(('grp', 'kv', 'sub'), 'hd'), parts along dimension 0, may hold values from -6 to 6
- suffix_pool_keys: bfloat16 [2048, 64, 1024], P(('grp', 'kv', 'sub'), None, 'hd'), parts along dimension 0, may hold values from -14 to 14
- suffix_pool_values: bfloat16 [2048, 64, 1024], P(('grp', 'kv', 'sub'), None, 'hd'), parts along dimension 0, may hold values from -6 to 6
Outputs:
- attended: float32 [256, 8192], P(('grp', 'kv'), 'hd'), parts along dimension 0
There are 2 independent parts, one for each index of `grp`. A program takes and returns all parts, laid end to end along the dimension named above; each array names one. Nothing has to cross between parts.
Inputs may be any that keep to these rules, and one draw needn't show every extreme that they name: `prompt_of`: in each aligned block of 16 rows (the sequences of one index of kv), every prompt is named by exactly 8 rows. `page_table`: for each index k of kv and s of sub, the entries in rows k * 16 to (k + 1) * 16 - 1 and columns s * 8 to (s + 1) * 8 - 1 are a permutation of 0 to 127.
All inputs are finite; a program needn't handle non-finite values.
Results may differ from a plain program's by a relative error of at most 0.0011.
Values may be sent and summed in bfloat16 or wider, within the bound.
No kernel may reach another device: no remote copies, remote signals or barrier semaphores. Data moves between devices by JAX's collectives and lax.ppermute only.
A program may use at most 128 MiB of HBM per device.

v0:
```python
import math
import jax
import jax.numpy as jnp
from jax import lax
from jax.sharding import PartitionSpec as P

HEAD_SIZE = 128
NEGATIVE = -1e30


def joined(value, axis, combine):
    everything = jax.tree.map(lambda part: lax.all_gather(part, axis), value)
    leading = jax.tree.map(lambda part: part[0], everything)

    def hop(k, so_far):
        return combine(so_far, jax.tree.map(lambda part: part[k], everything))

    return lax.fori_loop(1, lax.axis_size(axis), hop, leading)


def attend_block(sent_rows, key_block, value_block, lower_bound, upper_bound, first_position):
    row_count = sent_rows.shape[0]
    key_count = key_block.shape[0]
    kv_local = key_block.shape[1] // HEAD_SIZE
    query_group_size = sent_rows.shape[1] // (HEAD_SIZE * kv_local)
    position = first_position + jnp.arange(key_count, dtype=jnp.int32)
    key_mask = (position[None, :] >= lower_bound[:, None]) & (
        position[None, :] < upper_bound[:, None]
    )
    key_mask = key_mask[:, None, :]
    score_scale = 1.0 / math.sqrt(HEAD_SIZE)
    blended_parts = []
    lse_parts = []
    for kv_head in range(kv_local):
        low_column = kv_head * query_group_size * HEAD_SIZE
        head_query = sent_rows[:, low_column : low_column + query_group_size * HEAD_SIZE].reshape(
            row_count * query_group_size, HEAD_SIZE
        )
        head_keys = key_block[:, kv_head * HEAD_SIZE : (kv_head + 1) * HEAD_SIZE]
        head_values = value_block[:, kv_head * HEAD_SIZE : (kv_head + 1) * HEAD_SIZE]
        scores = lax.dot_general(
            head_query, head_keys, (((1,), (1,)), ((), ())), preferred_element_type=jnp.float32
        )
        scores = (scores * score_scale).reshape(row_count, query_group_size, key_count)
        scores = jnp.where(key_mask, scores, NEGATIVE)
        row_max = jnp.max(scores, axis=2, keepdims=True)
        weights = jnp.where(key_mask, jnp.exp(scores - row_max), 0.0)
        totals = jnp.maximum(jnp.sum(weights, axis=2), 1.0)
        weighted = jnp.dot(
            weights.astype(jnp.bfloat16).reshape(row_count * query_group_size, key_count),
            head_values,
            preferred_element_type=jnp.float32,
        )
        weighted = weighted.reshape(row_count, query_group_size, HEAD_SIZE) / totals[:, :, None]
        blended_parts.append(weighted.reshape(row_count, query_group_size * HEAD_SIZE))
        lse_parts.append(row_max[:, :, 0] + jnp.log(totals))
    return (jnp.concatenate(blended_parts, axis=1), jnp.concatenate(lse_parts, axis=1))


def combine_halves(earlier, later):
    joint_max = jnp.maximum(earlier[0], later[0])
    left_factor = jnp.exp(earlier[0] - joint_max)
    right_factor = jnp.exp(later[0] - joint_max)
    totals = earlier[1] * left_factor + later[1] * right_factor
    blended = earlier[2] * left_factor[:, :, None] + later[2] * right_factor[:, :, None]
    return (joint_max, totals, blended)


def shards(
    queries,
    prompt_of,
    prompt_len,
    suffix_len,
    page_table,
    prompt_keys,
    shared_prompt_values,
    suffix_pool_keys,
    suffix_pool_values,
):
    kv_count = lax.axis_size("kv")
    sub_count = lax.axis_size("sub")
    kv_index = lax.axis_index("kv")
    sub_index = lax.axis_index("sub")
    seq_local = queries.shape[0]
    row_width = queries.shape[1]
    heads_local = row_width // HEAD_SIZE
    cache_local = prompt_keys.shape[0]
    kv_reach = sub_count * cache_local
    prompt_count = prompt_len.shape[0]
    prompt_starts = jnp.cumsum(prompt_len) - prompt_len
    prompt_ends = prompt_starts + prompt_len
    prompt_labels = jnp.arange(prompt_count, dtype=jnp.int32)
    range_low = jnp.arange(kv_count, dtype=jnp.int32) * kv_reach
    intersections = (prompt_starts[None, :] < range_low[:, None] + kv_reach) & (
        prompt_ends[None, :] > range_low[:, None]
    )
    later_slot = prompt_starts[None, :] > range_low[:, None]
    first_position = (kv_index * sub_count + sub_index) * cache_local
    most_rows = seq_local // prompt_count
    owned_prompt = lax.dynamic_slice_in_dim(prompt_of[:, 0], kv_index * seq_local, seq_local)
    prompt_hits = owned_prompt[:, None] == prompt_labels[None, :]
    hit_counts = prompt_hits.astype(jnp.int32)
    ranks = jnp.sum((jnp.cumsum(hit_counts, axis=0) - hit_counts) * hit_counts, axis=1)
    seq_intersection = jnp.any(intersections[:, None, :] & prompt_hits[None, :, :], axis=2)
    seq_later = jnp.any(later_slot[:, None, :] & prompt_hits[None, :, :], axis=2).astype(jnp.int32)
    slot_labels = jnp.arange(2, dtype=jnp.int32)
    rank_labels = jnp.arange(most_rows, dtype=jnp.int32)
    selector = seq_intersection[:, None, None, :] & (
        seq_later[:, None, None, :] == slot_labels[None, :, None, None]
    )
    selector = selector & (ranks[None, None, None, :] == rank_labels[None, None, :, None])
    selector = selector.reshape(kv_count * 2 * most_rows, seq_local)
    outgoing = jnp.dot(
        selector.astype(jnp.bfloat16), queries, preferred_element_type=jnp.float32
    ).astype(jnp.bfloat16)
    incoming = lax.all_to_all(
        outgoing.reshape(kv_count, 2 * most_rows, row_width),
        "kv",
        split_axis=0,
        concat_axis=0,
        tiled=True,
    )
    mine_intersection = lax.dynamic_index_in_dim(intersections, kv_index, 0, keepdims=False)
    mine_later = lax.dynamic_index_in_dim(later_slot, kv_index, 0, keepdims=False).astype(jnp.int32)
    chosen = mine_intersection[None, :] & (mine_later[None, :] == slot_labels[:, None])
    slot_low = jnp.sum(jnp.where(chosen, prompt_starts[None, :], 0), axis=1)
    slot_high = jnp.sum(jnp.where(chosen, prompt_ends[None, :], 0), axis=1)
    lower_bound = jnp.broadcast_to(
        jnp.repeat(slot_low, most_rows)[None, :], (kv_count, 2 * most_rows)
    ).reshape(-1)
    upper_bound = jnp.broadcast_to(
        jnp.repeat(slot_high, most_rows)[None, :], (kv_count, 2 * most_rows)
    ).reshape(-1)
    sent_rows = incoming.reshape(kv_count * 2 * most_rows, row_width)
    back_rows = 2 * most_rows
    prompt_out, prompt_lse = attend_block(
        sent_rows, prompt_keys, shared_prompt_values, lower_bound, upper_bound, first_position
    )
    returned_out, returned_lse = (
        lax.all_to_all(
            prompt_out.reshape(kv_count, back_rows, row_width),
            "kv",
            split_axis=0,
            concat_axis=0,
            tiled=True,
        ),
        lax.all_to_all(
            prompt_lse.reshape(kv_count, back_rows, heads_local),
            "kv",
            split_axis=0,
            concat_axis=0,
            tiled=True,
        ),
    )
    page_slots = page_table.shape[1]
    page_length = suffix_pool_keys.shape[1]
    suffix_span = page_slots * page_length
    gathered_keys = suffix_pool_keys[page_table].reshape(seq_local, suffix_span, -1)
    gathered_values = suffix_pool_values[page_table].reshape(seq_local, suffix_span, -1)
    suffix_first = sub_index * suffix_span

    def one_sequence(query_line, seq_keys, seq_values, seq_length):
        return attend_block(
            query_line[None, :],
            seq_keys,
            seq_values,
            jnp.zeros((1,), jnp.int32),
            seq_length[None],
            suffix_first,
        )

    suffix_out, suffix_lse = jax.vmap(one_sequence)(
        queries, gathered_keys, gathered_values, suffix_len
    )
    suffix_out = suffix_out[:, 0].reshape(seq_local, heads_local, HEAD_SIZE)
    suffix_lse = suffix_lse[:, 0]
    flat_lse = returned_lse.reshape(-1, heads_local)
    flat_out = returned_out.reshape(-1, heads_local, HEAD_SIZE)
    masked_lse = jnp.where(selector[:, :, None], flat_lse[:, None, :], NEGATIVE)
    joint_max = jnp.maximum(jnp.max(masked_lse, axis=0), suffix_lse)
    factors = jnp.where(selector[:, :, None], jnp.exp(masked_lse - joint_max[None]), 0.0)
    own_factor = jnp.exp(suffix_lse - joint_max)
    totals = jnp.sum(factors, axis=0) + own_factor
    blended = jnp.einsum("rsh,rhd->shd", factors, flat_out, precision=lax.Precision.HIGHEST)
    blended = blended + own_factor[:, :, None] * suffix_out
    joint_max, totals, blended = joined((joint_max, totals, blended), "sub", combine_halves)
    return (blended / totals[:, :, None]).reshape(seq_local, row_width).astype(jnp.float32)


def solution(mesh):
    placed = (
        P(("grp", "kv"), "hd"),
        P("grp", None),
        P("grp"),
        P(("grp", "kv")),
        P(("grp", "kv"), "sub"),
        P(("grp", "kv", "sub"), "hd"),
        P(("grp", "kv", "sub"), "hd"),
        P(("grp", "kv", "sub"), None, "hd"),
        P(("grp", "kv", "sub"), None, "hd"),
    )
    return jax.shard_map(
        shards, mesh=mesh, in_specs=placed, out_specs=P(("grp", "kv"), "hd"), check_vma=False
    )
```

profile of v0, /device:TPU:0, one launch (start us, length us, event | category | flops | bytes accessed | tf_op | source)
XLA Modules:
  0.0 137.8 jit_solution(13117448288514897727)
XLA Ops:
  0.0 0.8 reduce-window.8
  2.4 2.3 %convolution_convert_fusion = bf16[128,4096]{1,0:T(8,128)(2,1)} fusion(pred[128,16]{1,0:T(8,128)(4,1)S(1)} %bitcast.195, bf16[16,4096]{1,0:T(8,128)(2,1)} %param.9), kind=kOutput, calls=%fused_computation.10 | convolution fusion | flops 17301504 | bytes 1181696 | tf_op jit(solution)/shard_map/dot_general | solution.py:113
  4.7 6.4 %all-to-all-start = ((bf16[8,16,4096]{2,1,0:T(8,128)(2,1)}), bf16[8,16,4096]{2,1,0:T(8,128)(2,1)S(1)}, u32[]{:S(2)}, u32[]{:S(2)}) async-start(bf16[8,16,4096]{2,1,0:T(8,128)(2,1)} %bitcast.7), calls=%async_computation | async-start | bytes 2097152 | tf_op jit(solution)/shard_map/all_to_all | solution.py:116
  12.7 0.8 slice_bitcast_fusion.1
  13.5 10.0 %gather_fusion.1 = bf16[128,64,512]{2,1,0:T(8,128)(2,1)} fusion(bf16[128,64,512]{2,1,0:T(8,128)(2,1)} %param.17, s32[1024]{0:T(1024)S(1)} %pad_clamp_fusion), kind=kCustom, calls=%fused_computation.1 | custom fusion | bytes 16777728 | tf_op jit(solution)/shard_map/gather | solution.py:159
  23.5 10.0 %gather_fusion = bf16[128,64,512]{2,1,0:T(8,128)(2,1)} fusion(bf16[128,64,512]{2,1,0:T(8,128)(2,1)} %param.16, s32[1024]{0:T(1024)S(1)} %pad_clamp_fusion), kind=kCustom, calls=%fused_computation | custom fusion | bytes 16777728 | tf_op jit(solution)/shard_map/gather | solution.py:158
  33.8 3.9 %all-to-all-done = bf16[8,16,4096]{2,1,0:T(8,128)(2,1)S(1)} async-done(((bf16[8,16,4096]{2,1,0:T(8,128)(2,1)}), bf16[8,16,4096]{2,1,0:T(8,128)(2,1)S(1)}, u32[]{:S(2)}, u32[]{:S(2)}) %all-to-all-start) | async-done | bytes 1048608 | tf_op jit(solution)/shard_map/all_to_all | solution.py:116
  38.1 2.6 %fusion.130 = f32[1024,1024]{1,0:T(8,128)} fusion(bf16[1024,128]{1,0:T(8,128)(2,1)S(1)} %reshape.707, bf16[1024,512]{1,0:T(8,128)(2,1)S(1)} %copy-done.6), kind=kOutput, calls=%fused_computation.99 | convolution fusion | flops 268435456 | bytes 4718592 | tf_op jit(solution)/shard_map/dot_general | solution.py:41
  40.7 2.7 %fusion.133 = f32[1024,1024]{1,0:T(8,128)} fusion(bf16[1024,128]{1,0:T(8,128)(2,1)S(1)} %reshape.706, bf16[1024,512]{1,0:T(8,128)(2,1)S(1)} %copy-done.6), kind=kOutput, calls=%fused_computation.102 | convolution fusion | flops 268435456 | bytes 4718592 | tf_op jit(solution)/shard_map/dot_general | solution.py:41
  43.5 1.2 fusion
  44.7 1.0 copy-done.2
  45.7 6.4 %fusion.4 = (f32[1024]{0:T(1024)S(1)}, f32[1024]{0:T(1024)S(1)}, f32[1024]{0:T(1024)S(1)}, f32[1024]{0:T(1024)S(1)}, f32[1024,1024]{1,0:T(8,128)S(1)}) fusion(f32[1024,1024]{1,0:T(8,128)S(1)} %get-tuple-element.51, f32[1024]{0:T(1024)S(1)} %get-tuple-element.50, pred[128,1024]{1,0:T(8,128)(4,1)S(1)} %compare_and_fusion, f32[1024,1024]{1,0:T(8,128)} %fusion.130, ...), kind=kOutput, calls=%fused_computation.15 | convolution fusion | flops 283111424 | bytes 17453056 | tf_op jit(solution)/shard_map/dot_general | solution.py:41
  52.1 5.0 %fusion.6 = (f32[1024]{0:T(1024)S(1)}, f32[1024]{0:T(1024)S(1)}, f32[1024]{0:T(1024)S(1)}) fusion(f32[1024,1024]{1,0:T(8,128)S(1)} %copy-done.2, f32[1024]{0:T(1024)S(1)} %get-tuple-element.8, pred[128,1024]{1,0:T(8,128)(4,1)S(1)} %compare_and_fusion, f32[1024]{0:T(1024)S(1)} %get-tuple-element.7, f32[1024,1024]{1,0:T(8,128)S(1)} %copy-done.3, ...), kind=kLoop, calls=%fused_computation.17 | loop fusion | flops 15725568 | bytes 12738560 | tf_op jit(solution)/shard_map/reduce_sum | solution.py:48
  57.2 3.4 %fusion.106 = f32[128,8,128]{2,1,0:T(8,128)S(1)} fusion(f32[1024,1024]{1,0:T(8,128)} %copy-done.5, f32[1024]{0:T(1024)S(1)} %get-tuple-element.6, pred[128,1024]{1,0:T(8,128)(4,1)S(1)} %compare_and_fusion, f32[128,8]{1,0:T(8,128)S(1)} %max.138, bf16[1024,512]{1,0:T(8,128)(2,1)} %param.15), kind=kOutput, calls=%fused_computation.74 | convolution fusion | flops 273809408 | bytes 5120000 | tf_op jit(solution)/shard_map/dot_general | solution.py:49
  60.8 3.2 %fusion.109 = f32[128,8,128]{2,1,0:T(8,128)S(1)} fusion(f32[1024,1024]{1,0:T(8,128)} %fusion.130, f32[1024]{0:T(1024)S(1)} %get-tuple-element.7, pred[128,1024]{1,0:T(8,128)(4,1)S(1)} %compare_and_fusion, f32[128,8]{1,0:T(8,128)S(1)} %max.136, bf16[1024,512]{1,0:T(8,128)(2,1)} %param.15), kind=kOutput, calls=%fused_computation.75 | convolution fusion | flops 273809408 | bytes 5120000 | tf_op jit(solution)/shard_map/dot_general | solution.py:49
  64.2 3.2 %fusion.112 = f32[128,8,128]{2,1,0:T(8,128)S(1)} fusion(f32[1024,1024]{1,0:T(8,128)} %fusion.133, f32[1024]{0:T(1024)S(1)} %get-tuple-element.8, pred[128,1024]{1,0:T(8,128)(4,1)S(1)} %compare_and_fusion, f32[128,8]{1,0:T(8,128)S(1)} %max.134, bf16[1024,512]{1,0:T(8,128)(2,1)} %param.15), kind=kOutput, calls=%fused_computation.76 | convolution fusion | flops 273809408 | bytes 5120000 | tf_op jit(solution)/shard_map/dot_general | solution.py:49
  67.6 3.2 %fusion.115 = f32[128,8,128]{2,1,0:T(8,128)S(1)} fusion(f32[1024,1024]{1,0:T(8,128)} %copy-done.4, f32[1024]{0:T(1024)S(1)} %get-tuple-element.50, pred[128,1024]{1,0:T(8,128)(4,1)S(1)} %compare_and_fusion, f32[128,8]{1,0:T(8,128)S(1)} %max.132, bf16[1024,512]{1,0:T(8,128)(2,1)} %param.15), kind=kOutput, calls=%fused_computation.77 | convolution fusion | flops 273809408 | bytes 5120000 | tf_op jit(solution)/shard_map/dot_general | solution.py:49
  72.1 3.3 %all-to-all-start.2 = ((f32[8,1,512]{2,1,0:T(1,128)}), f32[8,1,512]{2,1,0:T(1,128)S(1)}, u32[]{:S(2)}, u32[]{:S(2)}) async-start(f32[8,1,512]{2,1,0:T(1,128)} %reshape.747), calls=%async_computation.2 | async-start | bytes 32768 | tf_op jit(solution)/shard_map/all_to_all | solution.py:147
  75.4 1.5 %pad_maximum_fusion = f32[8,16,4096]{2,1,0:T(8,128)} fusion(f32[8,16,1024]{2,1,0:T(8,128)S(1)} %concatenate.25, f32[8,16,1024]{2,1,0:T(8,128)S(1)} %concatenate.24, f32[8,16,1024]{2,1,0:T(8,128)S(1)} %concatenate.23, f32[8,16,1024]{2,1,0:T(8,128)S(1)} %concatenate.22), kind=kLoop, calls=%fused_computation.43 | loop fusion | flops 1572864 | bytes 4194304 | tf_op jit(solution)/shard_map/concatenate | solution.py:57
  76.9 4.1 %all-to-all-done.2 = f32[8,1,512]{2,1,0:T(1,128)S(1)} async-done(((f32[8,1,512]{2,1,0:T(1,128)}), f32[8,1,512]{2,1,0:T(1,128)S(1)}, u32[]{:S(2)}, u32[]{:S(2)}) %all-to-all-start.2) | async-done | bytes 16416 | tf_op jit(solution)/shard_map/all_to_all | solution.py:147
  81.0 3.6 %all-to-all-start.1 = ((f32[8,16,4096]{2,1,0:T(8,128)}), f32[8,16,4096]{2,1,0:T(8,128)S(1)}, u32[]{:S(2)}, u32[]{:S(2)}) async-start(f32[8,16,4096]{2,1,0:T(8,128)} %pad_maximum_fusion), calls=%async_computation.1 | async-start | bytes 4194304 | tf_op jit(solution)/shard_map/all_to_all | solution.py:140
  84.6 2.3 %fusion.191 = (f32[16,8]{1,0:T(8,128)S(1)}, f32[16,8,512]{2,1,0:T(8,128)S(1)}) fusion(bf16[16,8,128]{2,1,0:T(8,128)(2,1)S(1)} %bitcast.206, bf16[16,512,512]{2,1,0:T(8,128)(2,1)} %bitcast.187, pred[16,512]{1,0:T(8,128)(4,1)S(1)} %iota_compare_fusion), kind=kOutput, calls=%fused_computation.201 | convolution fusion | flops 16973696 | bytes 2400768 | tf_op jit(solution)/shard_map/vmap()/dot_general | solution.py:41
  86.9 2.3 %fusion.192 = (f32[16,8]{1,0:T(8,128)S(1)}, f32[16,8,512]{2,1,0:T(8,128)S(1)}) fusion(bf16[16,8,128]{2,1,0:T(8,128)(2,1)S(1)} %bitcast.208, bf16[16,512,512]{2,1,0:T(8,128)(2,1)} %bitcast.188, pred[16,512]{1,0:T(8,128)(4,1)S(1)} %iota_compare_fusion), kind=kOutput, calls=%fused_computation.202 | convolution fusion | flops 16973696 | bytes 2400768 | tf_op jit(solution)/shard_map/vmap()/dot_general | solution.py:41
  89.3 2.3 %fusion.193 = (f32[16,8]{1,0:T(8,128)S(1)}, f32[16,8,512]{2,1,0:T(8,128)S(1)}) fusion(bf16[16,8,128]{2,1,0:T(8,128)(2,1)S(1)} %bitcast.207, bf16[16,512,512]{2,1,0:T(8,128)(2,1)} %bitcast.189, pred[16,512]{1,0:T(8,128)(4,1)S(1)} %iota_compare_fusion), kind=kOutput, calls=%fused_computation.203 | convolution fusion | flops 16973696 | bytes 2400768 | tf_op jit(solution)/shard_map/vmap()/dot_general | solution.py:41
  91.6 2.3 %fusion.194 = (f32[16,8]{1,0:T(8,128)S(1)}, f32[16,8,512]{2,1,0:T(8,128)S(1)}) fusion(bf16[16,8,128]{2,1,0:T(8,128)(2,1)S(1)} %bitcast.205, bf16[16,512,512]{2,1,0:T(8,128)(2,1)} %bitcast.190, pred[16,512]{1,0:T(8,128)(4,1)S(1)} %iota_compare_fusion), kind=kOutput, calls=%fused_computation.204 | convolution fusion | flops 16973696 | bytes 2400768 | tf_op jit(solution)/shard_map/vmap()/dot_general | solution.py:41
  94.3 2.0 %fusion.103 = f32[16,8,128]{2,1,0:T(8,128)S(1)} fusion(bf16[16,512,512]{2,1,0:T(8,128)(2,1)} %bitcast.183, f32[16,8,512]{2,1,0:T(8,128)S(1)} %get-tuple-element.54, f32[16,8]{1,0:T(8,128)S(1)} %get-tuple-element.53, pred[16,512]{1,0:T(8,128)(4,1)S(1)} %iota_compare_fusion, f32[16,8]{1,0:T(8,128)S(1)} %get-tuple-element.37), kind=kOutput, calls=%fused_computation.73 | convolution fusion | flops 16990208 | bytes 2434048 | tf_op jit(solution)/shard_map/vmap()/dot_general | solution.py:49
  96.4 2.0 %fusion.100 = f32[16,8,128]{2,1,0:T(8,128)S(1)} fusion(bf16[16,512,512]{2,1,0:T(8,128)(2,1)} %bitcast.184, f32[16,8,512]{2,1,0:T(8,128)S(1)} %get-tuple-element.60, f32[16,8]{1,0:T(8,128)S(1)} %get-tuple-element.59, pred[16,512]{1,0:T(8,128)(4,1)S(1)} %iota_compare_fusion, f32[16,8]{1,0:T(8,128)S(1)} %get-tuple-element.63), kind=kOutput, calls=%fused_computation.72 | convolution fusion | flops 16990208 | bytes 2434048 | tf_op jit(solution)/shard_map/vmap()/dot_general | solution.py:49
  98.5 2.0 %fusion.97 = f32[16,8,128]{2,1,0:T(8,128)S(1)} fusion(bf16[16,512,512]{2,1,0:T(8,128)(2,1)} %bitcast.185, f32[16,8,512]{2,1,0:T(8,128)S(1)} %get-tuple-element.58, f32[16,8]{1,0:T(8,128)S(1)} %get-tuple-element.57, pred[16,512]{1,0:T(8,128)(4,1)S(1)} %iota_compare_fusion, f32[16,8]{1,0:T(8,128)S(1)} %get-tuple-element.33), kind=kOutput, calls=%fused_computation.71 | convolution fusion | flops 16990208 | bytes 2434048 | tf_op jit(solution)/shard_map/vmap()/dot_general | solution.py:49
  100.5 2.0 %fusion.94 = f32[16,8,128]{2,1,0:T(8,128)S(1)} fusion(bf16[16,512,512]{2,1,0:T(8,128)(2,1)} %bitcast.186, f32[16,8,512]{2,1,0:T(8,128)S(1)} %get-tuple-element.56, f32[16,8]{1,0:T(8,128)S(1)} %get-tuple-element.55, pred[16,512]{1,0:T(8,128)(4,1)S(1)} %iota_compare_fusion, f32[16,8]{1,0:T(8,128)S(1)} %get-tuple-element.65), kind=kOutput, calls=%fused_computation.70 | convolution fusion | flops 16990208 | bytes 2434048 | tf_op jit(solution)/shard_map/vmap()/dot_general | solution.py:49
  104.8 28.8 %all-to-all-done.1 = f32[8,16,4096]{2,1,0:T(8,128)S(1)} async-done(((f32[8,16,4096]{2,1,0:T(8,128)}), f32[8,16,4096]{2,1,0:T(8,128)S(1)}, u32[]{:S(2)}, u32[]{:S(2)}) %all-to-all-start.1) | async-done | bytes 2097184 | tf_op jit(solution)/shard_map/all_to_all | solution.py:140
  133.9 3.1 %fusion.55 = f32[32,2,8,128]{3,2,1,0:T(8,128)S(1)} fusion(f32[128,32,128]{2,1,0:T(8,128)S(1)} %bitcast.182, f32[16,32,128]{2,1,0:T(8,128)S(1)} %bitcast.192, f32[16,32]{0,1:T(8,128)S(1)} %get-tuple-element.20, f32[16,32]{0,1:T(8,128)S(1)} %get-tuple-element.21, f32[16,32]{0,1:T(8,128)S(1)} %fusion.167, f32[128,32]{0,1:T(8,128)S(1)} %copy.63, ...), kind=kOutput, calls=%fused_computation.57 | convolution fusion | flops 101056512 | bytes 2646016 | tf_op jit(solution)/shard_map/rsh,rhd->shd/dot_general | solution.py:184
  137.1 0.7 copy.93
  (98 shorter events, 8.8 us)
Async XLA Ops:
  0.0 1.5 %copy-start = (s32[128,1]{0,1:T(1,128)S(1)}, s32[128,1]{0,1:T(1,128)}, u32[]{:S(2)}) copy-start(s32[128,1]{0,1:T(1,128)} %param.10) | copy-start | bytes 1540
  4.7 32.9 %all-to-all-start = ((bf16[8,16,4096]{2,1,0:T(8,128)(2,1)}), bf16[8,16,4096]{2,1,0:T(8,128)(2,1)S(1)}, u32[]{:S(2)}, u32[]{:S(2)}) async-start(bf16[8,16,4096]{2,1,0:T(8,128)(2,1)} %bitcast.7), calls=%async_computation | async-start | bytes 2097152 | tf_op jit(solution)/shard_map/all_to_all | solution.py:116
  23.5 10.0 %copy-start.7 = (s32[16]{0:T(128)S(1)}, s32[16]{0:T(128)}, u32[]{:S(2)}) copy-start(s32[16]{0:T(128)} %param.12) | copy-start | bytes 196
  33.4 4.6 %copy-start.6 = (bf16[1024,512]{1,0:T(8,128)(2,1)S(1)}, bf16[1024,512]{1,0:T(8,128)(2,1)}, u32[]{:S(2)}) copy-start(bf16[1024,512]{1,0:T(8,128)(2,1)} %param.14) | copy-start | bytes 3145732
  43.5 2.2 %copy-start.2 = (f32[1024,1024]{1,0:T(8,128)S(1)}, f32[1024,1024]{1,0:T(8,128)}, u32[]{:S(2)}) copy-start(f32[1024,1024]{1,0:T(8,128)} %fusion.133) | copy-start | bytes 12582916
  44.7 7.4 %copy-start.4 = (f32[1024,1024]{1,0:T(8,128)}, f32[1024,1024]{1,0:T(8,128)S(1)}, u32[]{:S(2)}) copy-start(f32[1024,1024]{1,0:T(8,128)S(1)} %get-tuple-element.51) | copy-start | bytes 12582916
  45.7 6.4 %copy-start.3 = (f32[1024,1024]{1,0:T(8,128)S(1)}, f32[1024,1024]{1,0:T(8,128)}, u32[]{:S(2)}) copy-start(f32[1024,1024]{1,0:T(8,128)} %fusion.130) | copy-start | bytes 12582916
  52.1 5.0 %copy-start.5 = (f32[1024,1024]{1,0:T(8,128)}, f32[1024,1024]{1,0:T(8,128)S(1)}, u32[]{:S(2)}) copy-start(f32[1024,1024]{1,0:T(8,128)S(1)} %get-tuple-element.52) | copy-start | bytes 12582916
  72.1 8.9 %all-to-all-start.2 = ((f32[8,1,512]{2,1,0:T(1,128)}), f32[8,1,512]{2,1,0:T(1,128)S(1)}, u32[]{:S(2)}, u32[]{:S(2)}) async-start(f32[8,1,512]{2,1,0:T(1,128)} %reshape.747), calls=%async_computation.2 | async-start | bytes 32768 | tf_op jit(solution)/shard_map/all_to_all | solution.py:147
  81.0 52.6 %all-to-all-start.1 = ((f32[8,16,4096]{2,1,0:T(8,128)}), f32[8,16,4096]{2,1,0:T(8,128)S(1)}, u32[]{:S(2)}, u32[]{:S(2)}) async-start(f32[8,16,4096]{2,1,0:T(8,128)} %pad_maximum_fusion), calls=%async_computation.1 | async-start | bytes 4194304 | tf_op jit(solution)/shard_map/all_to_all | solution.py:140
  102.6 35.2 %copy-start.1 = (s32[128,1]{0,1:T(1,128)S(1)}, s32[128,1]{0,1:T(1,128)}, u32[]{:S(2)}) copy-start(s32[128,1]{0,1:T(1,128)} %param.10) | copy-start | bytes 1540
where the time goes:
time: 139 us; the launch traced here: 138 us
  matrix products  48.7 us (35%)
  waiting for transfers between devices  36.7 us (26%)
  local copies, waits for them, and re-layouts  27.3 us (20%)
  starting transfers between devices  13.3 us (10%)
  other arithmetic  11.3 us (8%)
    all_to_all x1, waiting for transfers between devices, shards(): lax.all_to_all(prompt_out.reshape(kv_count, back_rows, row_width), 'kv',...  28.8 us
    dot_general x8, matrix products, attend_block(): lax.dot_general(head_query, head_keys, (((1,), (1,)), ((), ())), preferre...  22.2 us
    dot_general x8, matrix products, attend_block(): jnp.dot(weights.astype(jnp.bfloat16).reshape(row_count * query_group_size...  21.1 us
    gather x1, local copies, waits for them, and re-layouts, shards(): suffix_pool_values[page_table].reshape(seq_local, suffix_span, -1)  9.96 us
    gather x1, local copies, waits for them, and re-layouts, shards(): suffix_pool_keys[page_table].reshape(seq_local, suffix_span, -1)  9.96 us
    all_to_all x1, starting transfers between devices, shards(): lax.all_to_all(outgoing.reshape(kv_count, 2 * most_rows, row_width), 'kv'...  6.37 us
    reduce_sum x2, other arithmetic, attend_block(): totals = jnp.maximum(jnp.sum(weights, axis=2), 1.0)  5.36 us
    all_to_all x1, waiting for transfers between devices, shards(): lax.all_to_all(prompt_lse.reshape(kv_count, back_rows, heads_local), 'kv'...  4.09 us
  transfers between devices with their start and end apart: 3, of which 3 were waited for; matrix products, arithmetic and copies ran while one was open for 32% of the time, Pallas kernels for 0%

commit v1 on v0

--- a/solution.py
+++ b/solution.py
@@ -6,6 +6,28 @@
 
 HEAD_SIZE = 128
 NEGATIVE = -1e30
+
+
+def split_up(array, dim, peers):
+    before, after = (array.shape[:dim], array.shape[dim + 1 :])
+    return jnp.moveaxis(array.reshape(*before, peers, -1, *after), dim, 0)
+
+
+def in_order(blocks, dim):
+    shape = list(blocks.shape[1:])
+    shape[dim] *= blocks.shape[0]
+    return jnp.moveaxis(blocks, 0, dim).reshape(shape)
+
+
+def pairwise_exchange(x, axis, split_dim, concat_dim):
+    size, mine = (lax.axis_size(axis), lax.axis_index(axis))
+    blocks = split_up(x, split_dim, size)
+    outs = [blocks[mine]]
+    for lap in range(1, size):
+        sent = blocks[mine ^ lap]
+        outs.append(lax.ppermute(sent, axis, [(i, i ^ lap) for i in range(size)]))
+    blocks = jnp.stack(outs)[mine ^ jnp.arange(size)]
+    return in_order(blocks, concat_dim)
 
 
 def joined(value, axis, combine):
@@ -144,13 +166,7 @@
             concat_axis=0,
             tiled=True,
         ),
-        lax.all_to_all(
-            prompt_lse.reshape(kv_count, back_rows, heads_local),
-            "kv",
-            split_axis=0,
-            concat_axis=0,
-            tiled=True,
-        ),
+        pairwise_exchange(prompt_lse.reshape(kv_count, back_rows, heads_local), "kv", 0, 0),
     )
     page_slots = page_table.shape[1]
     page_length = suffix_pool_keys.shape[1]

time: 139 us -> 145 us (1.043)
  starting transfers between devices: 13.3 us -> 22.4 us
  waiting for transfers between devices: 36.7 us -> 31.9 us
    ppermute x0 -> x7, waiting for transfers between devices: none -> 31.9 us  [pairwise_exchange(): outs.append(lax.ppermute(sent, axis, [(i, i ^ lap) for i in range(size)]))]
    all_to_all x1, waiting for transfers between devices: 28.8 us -> 0.01 us  [shards(): lax.all_to_all(prompt_out.reshape(kv_count, back_rows, row_width), 'kv',...]
    ppermute x0 -> x7, starting transfers between devices: none -> 10.8 us  [pairwise_exchange(): outs.append(lax.ppermute(sent, axis, [(i, i ^ lap) for i in range(size)]))]
    all_to_all x1 -> x0, waiting for transfers between devices: 4.09 us -> none  [shards(): lax.all_to_all(prompt_lse.reshape(kv_count, back_rows, heads_local), 'kv'...]
    all_to_all x1, waiting for transfers between devices: 3.86 us -> 0.01 us  [shards(): lax.all_to_all(outgoing.reshape(kv_count, 2 * most_rows, row_width), 'kv'...]
    all_to_all x1 -> x0, starting transfers between devices: 3.34 us -> none  [shards(): lax.all_to_all(prompt_lse.reshape(kv_count, back_rows, heads_local), 'kv'...]
    all_to_all x1, starting transfers between devices: 3.6 us -> 5.24 us  [shards(): lax.all_to_all(prompt_out.reshape(kv_count, back_rows, row_width), 'kv',...]
    unnamed x25 -> x69, local copies, waits for them, and re-layouts: 3.06 us -> 2.98 us
  transfers between devices with their start and end apart: 3 -> 9, of which waited for: 3 -> 2; matrix products, arithmetic and copies ran while one was open for 32% -> 31% of each run, Pallas kernels for 0% -> 0%
where the time goes in v1:
time: 145 us; the launch traced here: 144 us
  matrix products  49.8 us (34%)
  waiting for transfers between devices  31.9 us (22%)
  local copies, waits for them, and re-layouts  27.2 us (19%)
  starting transfers between devices  22.4 us (15%)
  other arithmetic  11.9 us (8%)
    ppermute x7, waiting for transfers between devices, pairwise_exchange(): outs.append(lax.ppermute(sent, axis, [(i, i ^ lap) for i in range(size)]))  31.9 us
    dot_general x8, matrix products, attend_block(): lax.dot_general(head_query, head_keys, (((1,), (1,)), ((), ())), preferre...  22.9 us
    dot_general x8, matrix products, attend_block(): jnp.dot(weights.astype(jnp.bfloat16).reshape(row_count * query_group_size...  21.5 us
    ppermute x7, starting transfers between devices, pairwise_exchange(): outs.append(lax.ppermute(sent, axis, [(i, i ^ lap) for i in range(size)]))  10.8 us
    gather x1, local copies, waits for them, and re-layouts, shards(): suffix_pool_values[page_table].reshape(seq_local, suffix_span, -1)  9.96 us
    gather x1, local copies, waits for them, and re-layouts, shards(): suffix_pool_keys[page_table].reshape(seq_local, suffix_span, -1)  9.96 us
    all_to_all x1, starting transfers between devices, shards(): lax.all_to_all(outgoing.reshape(kv_count, 2 * most_rows, row_width), 'kv'...  6.36 us
    reduce_sum x2, other arithmetic, attend_block(): totals = jnp.maximum(jnp.sum(weights, axis=2), 1.0)  6.07 us
  transfers between devices with their start and end apart: 9, of which 2 were waited for; matrix products, arithmetic and copies ran while one was open for 31% of the time, Pallas kernels for 0%

profile of v1, /device:TPU:0, one launch (start us, length us, event | category | flops | bytes accessed | tf_op | source)
XLA Modules:
  0.0 144.1 jit_solution(11416951424150058848)
XLA Ops:
  3.0 2.3 %convolution_convert_fusion = bf16[128,4096]{1,0:T(8,128)(2,1)} fusion(pred[128,16]{1,0:T(8,128)(4,1)S(1)} %bitcast.226, bf16[16,4096]{1,0:T(8,128)(2,1)} %param.9), kind=kOutput, calls=%fused_computation.11 | convolution fusion | flops 17301504 | bytes 1181696 | tf_op jit(solution)/shard_map/dot_general | solution.py:135
  5.3 6.4 %all-to-all-start = ((bf16[8,16,4096]{2,1,0:T(8,128)(2,1)}), bf16[8,16,4096]{2,1,0:T(8,128)(2,1)S(1)}, u32[]{:S(2)}, u32[]{:S(2)}) async-start(bf16[8,16,4096]{2,1,0:T(8,128)(2,1)} %bitcast.7), calls=%async_computation | async-start | bytes 2097152 | tf_op jit(solution)/shard_map/all_to_all | solution.py:138
  14.0 10.0 %gather_fusion.2 = bf16[128,64,512]{2,1,0:T(8,128)(2,1)} fusion(bf16[128,64,512]{2,1,0:T(8,128)(2,1)} %param.17, s32[1024]{0:T(1024)S(1)} %pad_clamp_fusion), kind=kCustom, calls=%fused_computation.2 | custom fusion | bytes 16777728 | tf_op jit(solution)/shard_map/gather | solution.py:175
  24.0 10.0 %gather_fusion.1 = bf16[128,64,512]{2,1,0:T(8,128)(2,1)} fusion(bf16[128,64,512]{2,1,0:T(8,128)(2,1)} %param.16, s32[1024]{0:T(1024)S(1)} %pad_clamp_fusion), kind=kCustom, calls=%fused_computation.1 | custom fusion | bytes 16777728 | tf_op jit(solution)/shard_map/gather | solution.py:174
  34.1 2.3 %fusion.194 = (f32[16,8]{1,0:T(8,128)S(1)}, f32[16,8,512]{2,1,0:T(8,128)S(1)}) fusion(bf16[16,8,128]{2,1,0:T(8,128)(2,1)S(1)} %bitcast.239, bf16[16,512,512]{2,1,0:T(8,128)(2,1)} %bitcast.218, pred[16,512]{1,0:T(8,128)(4,1)S(1)} %iota_compare_fusion), kind=kOutput, calls=%fused_computation.222 | convolution fusion | flops 16973696 | bytes 2400768 | tf_op jit(solution)/shard_map/vmap()/dot_general | solution.py:63
  36.4 2.3 %fusion.195 = (f32[16,8]{1,0:T(8,128)S(1)}, f32[16,8,512]{2,1,0:T(8,128)S(1)}) fusion(bf16[16,8,128]{2,1,0:T(8,128)(2,1)S(1)} %bitcast.240, bf16[16,512,512]{2,1,0:T(8,128)(2,1)} %bitcast.219, pred[16,512]{1,0:T(8,128)(4,1)S(1)} %iota_compare_fusion), kind=kOutput, calls=%fused_computation.223 | convolution fusion | flops 16973696 | bytes 2400768 | tf_op jit(solution)/shard_map/vmap()/dot_general | solution.py:63
  38.7 2.3 %fusion.196 = (f32[16,8]{1,0:T(8,128)S(1)}, f32[16,8,512]{2,1,0:T(8,128)S(1)}) fusion(bf16[16,8,128]{2,1,0:T(8,128)(2,1)S(1)} %bitcast.238, bf16[16,512,512]{2,1,0:T(8,128)(2,1)} %bitcast.220, pred[16,512]{1,0:T(8,128)(4,1)S(1)} %iota_compare_fusion), kind=kOutput, calls=%fused_computation.224 | convolution fusion | flops 16973696 | bytes 2400768 | tf_op jit(solution)/shard_map/vmap()/dot_general | solution.py:63
  41.0 2.4 %fusion.197 = (f32[16,8]{1,0:T(8,128)S(1)}, f32[16,8,512]{2,1,0:T(8,128)S(1)}) fusion(bf16[16,8,128]{2,1,0:T(8,128)(2,1)S(1)} %bitcast.237, bf16[16,512,512]{2,1,0:T(8,128)(2,1)} %bitcast.221, pred[16,512]{1,0:T(8,128)(4,1)S(1)} %iota_compare_fusion), kind=kOutput, calls=%fused_computation.225 | convolution fusion | flops 16973696 | bytes 2400768 | tf_op jit(solution)/shard_map/vmap()/dot_general | solution.py:63
  43.5 0.9 fusion.139
  45.2 2.7 %fusion.103 = f32[16,8,128]{2,1,0:T(8,128)} fusion(bf16[16,512,512]{2,1,0:T(8,128)(2,1)} %bitcast.214, f32[16,8,512]{2,1,0:T(8,128)S(1)} %get-tuple-element.62, f32[16,8]{1,0:T(8,128)S(1)} %get-tuple-element.61, pred[16,512]{1,0:T(8,128)(4,1)S(1)} %iota_compare_fusion, f32[16,8]{1,0:T(8,128)S(1)} %get-tuple-element.45), kind=kOutput, calls=%fused_computation.74 | convolution fusion | flops 16990208 | bytes 2434048 | tf_op jit(solution)/shard_map/vmap()/dot_general | solution.py:71
  48.3 2.7 %fusion.130 = f32[1024,1024]{1,0:T(8,128)} fusion(bf16[1024,128]{1,0:T(8,128)(2,1)S(1)} %reshape.806, bf16[1024,512]{1,0:T(8,128)(2,1)S(1)} %copy-done.6), kind=kOutput, calls=%fused_computation.100 | convolution fusion | flops 268435456 | bytes 4718592 | tf_op jit(solution)/shard_map/dot_general | solution.py:63
  51.0 2.6 %fusion.133 = f32[1024,1024]{1,0:T(8,128)} fusion(bf16[1024,128]{1,0:T(8,128)(2,1)S(1)} %reshape.805, bf16[1024,512]{1,0:T(8,128)(2,1)S(1)} %copy-done.6), kind=kOutput, calls=%fused_computation.103 | convolution fusion | flops 268435456 | bytes 4718592 | tf_op jit(solution)/shard_map/dot_general | solution.py:63
  53.8 1.2 fusion
  55.0 1.0 copy-done.2
  56.0 7.0 %fusion.4 = (f32[1024]{0:T(1024)}, f32[1024]{0:T(1024)S(1)}, f32[1024]{0:T(1024)S(1)}, f32[1024]{0:T(1024)S(1)}, f32[1024,1024]{1,0:T(8,128)S(1)}) fusion(f32[1024,1024]{1,0:T(8,128)S(1)} %get-tuple-element.59, f32[1024]{0:T(1024)S(1)} %get-tuple-element.58, pred[128,1024]{1,0:T(8,128)(4,1)S(1)} %compare_and_fusion, f32[1024,1024]{1,0:T(8,128)} %fusion.130, ...), kind=kOutput, calls=%fused_computation.16 | convolution fusion | flops 283111424 | bytes 17453056 | tf_op jit(solution)/shard_map/dot_general | solution.py:63
  62.9 5.2 %fusion.6 = (f32[1024]{0:T(1024)S(1)}, f32[1024]{0:T(1024)S(1)}, f32[1024]{0:T(1024)S(1)}) fusion(f32[1024,1024]{1,0:T(8,128)S(1)} %copy-done.2, f32[1024]{0:T(1024)S(1)} %get-tuple-element.8, pred[128,1024]{1,0:T(8,128)(4,1)S(1)} %compare_and_fusion, f32[1024]{0:T(1024)S(1)} %get-tuple-element.7, f32[1024,1024]{1,0:T(8,128)S(1)} %copy-done.3, ...), kind=kLoop, calls=%fused_computation.18 | loop fusion | flops 15725568 | bytes 12738560 | tf_op jit(solution)/shard_map/reduce_sum | solution.py:70
  68.2 3.2 %fusion.106 = f32[128,8,128]{2,1,0:T(8,128)S(1)} fusion(f32[1024,1024]{1,0:T(8,128)} %copy-done.5, f32[1024]{0:T(1024)S(1)} %get-tuple-element.6, pred[128,1024]{1,0:T(8,128)(4,1)S(1)} %compare_and_fusion, f32[128,8]{1,0:T(8,128)S(1)} %max.162, bf16[1024,512]{1,0:T(8,128)(2,1)S(1)} %copy-done.27), kind=kOutput, calls=%fused_computation.75 | convolution fusion | flops 273809408 | bytes 5181440 | tf_op jit(solution)/shard_map/dot_general | solution.py:71
  71.6 3.2 %fusion.109 = f32[128,8,128]{2,1,0:T(8,128)S(1)} fusion(f32[1024,1024]{1,0:T(8,128)} %fusion.130, f32[1024]{0:T(1024)S(1)} %get-tuple-element.7, pred[128,1024]{1,0:T(8,128)(4,1)S(1)} %compare_and_fusion, f32[128,8]{1,0:T(8,128)S(1)} %max.160, bf16[1024,512]{1,0:T(8,128)(2,1)S(1)} %copy-done.27), kind=kOutput, calls=%fused_computation.76 | convolution fusion | flops 273809408 | bytes 5181440 | tf_op jit(solution)/shard_map/dot_general | solution.py:71
  75.0 3.2 %fusion.112 = f32[128,8,128]{2,1,0:T(8,128)S(1)} fusion(f32[1024,1024]{1,0:T(8,128)} %fusion.133, f32[1024]{0:T(1024)S(1)} %get-tuple-element.8, pred[128,1024]{1,0:T(8,128)(4,1)S(1)} %compare_and_fusion, f32[128,8]{1,0:T(8,128)S(1)} %max.158, bf16[1024,512]{1,0:T(8,128)(2,1)} %param.15), kind=kOutput, calls=%fused_computation.77 | convolution fusion | flops 273809408 | bytes 5120000 | tf_op jit(solution)/shard_map/dot_general | solution.py:71
  78.4 3.2 %fusion.115 = f32[128,8,128]{2,1,0:T(8,128)S(1)} fusion(f32[1024,1024]{1,0:T(8,128)} %copy-done.4, f32[1024]{0:T(1024)S(1)} %get-tuple-element.58, pred[128,1024]{1,0:T(8,128)(4,1)S(1)} %compare_and_fusion, f32[128,8]{1,0:T(8,128)S(1)} %max.156, bf16[1024,512]{1,0:T(8,128)(2,1)} %param.15), kind=kOutput, calls=%fused_computation.78 | convolution fusion | flops 273809408 | bytes 5120000 | tf_op jit(solution)/shard_map/dot_general | solution.py:71
  81.8 1.5 %pad_maximum_fusion = f32[8,16,4096]{2,1,0:T(8,128)} fusion(f32[8,16,1024]{2,1,0:T(8,128)S(1)} %concatenate.25, f32[8,16,1024]{2,1,0:T(8,128)S(1)} %concatenate.24, f32[8,16,1024]{2,1,0:T(8,128)S(1)} %concatenate.23, f32[8,16,1024]{2,1,0:T(8,128)S(1)} %concatenate.22), kind=kLoop, calls=%fused_computation.44 | loop fusion | flops 1572864 | bytes 4194304 | tf_op jit(solution)/shard_map/concatenate | solution.py:79
  83.3 5.2 %all-to-all-start.1 = ((f32[8,16,4096]{2,1,0:T(8,128)}), f32[8,16,4096]{2,1,0:T(8,128)S(1)}, u32[]{:S(2)}, u32[]{:S(2)}) async-start(f32[8,16,4096]{2,1,0:T(8,128)} %pad_maximum_fusion), calls=%async_computation.1 | async-start | bytes 4194304 | tf_op jit(solution)/shard_map/all_to_all | solution.py:162
  88.6 2.0 %fusion.100 = f32[16,8,128]{2,1,0:T(8,128)S(1)} fusion(bf16[16,512,512]{2,1,0:T(8,128)(2,1)} %bitcast.215, f32[16,8,512]{2,1,0:T(8,128)S(1)} %copy-done.10, f32[16,8]{1,0:T(8,128)S(1)} %copy-done.21, pred[16,512]{1,0:T(8,128)(4,1)S(1)} %iota_compare_fusion, f32[16,8]{1,0:T(8,128)S(1)} %copy-done.24), kind=kOutput, calls=%fused_computation.73 | convolution fusion | flops 16990208 | bytes 2434048 | tf_op jit(solution)/shard_map/vmap()/dot_general | solution.py:71
  90.8 2.0 %fusion.97 = f32[16,8,128]{2,1,0:T(8,128)S(1)} fusion(bf16[16,512,512]{2,1,0:T(8,128)(2,1)} %bitcast.216, f32[16,8,512]{2,1,0:T(8,128)S(1)} %copy-done.8, f32[16,8]{1,0:T(8,128)S(1)} %copy-done.17, pred[16,512]{1,0:T(8,128)(4,1)S(1)} %iota_compare_fusion, f32[16,8]{1,0:T(8,128)S(1)} %get-tuple-element.41), kind=kOutput, calls=%fused_computation.72 | convolution fusion | flops 16990208 | bytes 2434048 | tf_op jit(solution)/shard_map/vmap()/dot_general | solution.py:71
  92.9 2.0 %fusion.94 = f32[16,8,128]{2,1,0:T(8,128)S(1)} fusion(bf16[16,512,512]{2,1,0:T(8,128)(2,1)} %bitcast.217, f32[16,8,512]{2,1,0:T(8,128)S(1)} %get-tuple-element.64, f32[16,8]{1,0:T(8,128)S(1)} %copy-done.15, pred[16,512]{1,0:T(8,128)(4,1)S(1)} %iota_compare_fusion, f32[16,8]{1,0:T(8,128)S(1)} %get-tuple-element.73), kind=kOutput, calls=%fused_computation.71 | convolution fusion | flops 16990208 | bytes 2434048 | tf_op jit(solution)/shard_map/vmap()/dot_general | solution.py:71
  96.6 1.6 %collective-permute-start.1 = (f32[1,16,32]{2,1,0:T(8,128)S(1)}, f32[1,16,32]{2,1,0:T(8,128)S(1)}, u32[]{:S(2)}, u32[]{:S(2)}) collective-permute-start(f32[1,16,32]{2,1,0:T(8,128)S(1)} %get-tuple-element.35), channel_id=1, source_target_pairs={{0,4},{2,6},{4,0},{6,2},{8,12},{10,14},{12,8},{14,10},{1,5},{3,7},... | collective-permute-start | bytes 6152 | tf_op jit(solution)/shard_map/ppermute | solution.py:28
  98.2 2.6 %collective-permute-start.3 = (f32[1,16,32]{2,1,0:T(8,128)S(1)}, f32[1,16,32]{2,1,0:T(8,128)S(1)}, u32[]{:S(2)}, u32[]{:S(2)}) collective-permute-start(f32[1,16,32]{2,1,0:T(8,128)S(1)} %get-tuple-element.33), channel_id=1, source_target_pairs={{0,8},{2,10},{4,12},{6,14},{8,0},{10,2},{12,4},{14,6},{1,9},{3,11}... | collective-permute-start | bytes 6152 | tf_op jit(solution)/shard_map/ppermute | solution.py:28
  101.0 3.4 %collective-permute-start.5 = (f32[1,16,32]{2,1,0:T(8,128)S(1)}, f32[1,16,32]{2,1,0:T(8,128)S(1)}, u32[]{:S(2)}, u32[]{:S(2)}) collective-permute-start(f32[1,16,32]{2,1,0:T(8,128)S(1)} %get-tuple-element.31), channel_id=1, source_target_pairs={{0,12},{2,14},{4,8},{6,10},{8,4},{10,6},{12,0},{14,2},{1,13},{3,15... | collective-permute-start | bytes 6152 | tf_op jit(solution)/shard_map/ppermute | solution.py:28
  104.4 19.4 %collective-permute-done.1 = f32[1,16,32]{2,1,0:T(8,128)S(1)} collective-permute-done((f32[1,16,32]{2,1,0:T(8,128)S(1)}, f32[1,16,32]{2,1,0:T(8,128)S(1)}, u32[]{:S(2)}, u32[]{:S(2)}) %collective-permute-start.1) | collective-permute-done | bytes 2080 | tf_op jit(solution)/shard_map/ppermute | solution.py:28
  123.8 2.4 %collective-permute-start.6 = (f32[1,16,32]{2,1,0:T(8,128)S(1)}, f32[1,16,32]{2,1,0:T(8,128)S(1)}, u32[]{:S(2)}, u32[]{:S(2)}) collective-permute-start(f32[1,16,32]{2,1,0:T(8,128)S(1)} %get-tuple-element.30), channel_id=1, source_target_pairs={{0,14},{2,12},{4,10},{6,8},{8,6},{10,4},{12,2},{14,0},{1,15},{3,13... | collective-permute-start | bytes 6152 | tf_op jit(solution)/shard_map/ppermute | solution.py:28
  126.2 12.5 %collective-permute-done.3 = f32[1,16,32]{2,1,0:T(8,128)S(1)} collective-permute-done((f32[1,16,32]{2,1,0:T(8,128)S(1)}, f32[1,16,32]{2,1,0:T(8,128)S(1)}, u32[]{:S(2)}, u32[]{:S(2)}) %collective-permute-start.3) | collective-permute-done | bytes 2080 | tf_op jit(solution)/shard_map/ppermute | solution.py:28
  140.3 3.1 %fusion.55 = f32[32,2,8,128]{3,2,1,0:T(8,128)S(1)} fusion(f32[128,32,128]{2,1,0:T(8,128)S(1)} %bitcast.213, f32[16,32,128]{2,1,0:T(8,128)S(1)} %bitcast.223, f32[16,32]{0,1:T(8,128)S(1)} %get-tuple-element.20, f32[16,32]{0,1:T(8,128)S(1)} %get-tuple-element.21, f32[16,32]{0,1:T(8,128)S(1)} %fusion.167, f32[128,32]{0,1:T(8,128)S(1)} %copy.63, ...), kind=kOutput, calls=%fused_computation.58 | convolution fusion | flops 101056512 | bytes 2646016 | tf_op jit(solution)/shard_map/rsh,rhd->shd/dot_general | solution.py:200
  (157 shorter events, 11.4 us)
Async XLA Ops:
  5.3 42.6 %all-to-all-start = ((bf16[8,16,4096]{2,1,0:T(8,128)(2,1)}), bf16[8,16,4096]{2,1,0:T(8,128)(2,1)S(1)}, u32[]{:S(2)}, u32[]{:S(2)}) async-start(bf16[8,16,4096]{2,1,0:T(8,128)(2,1)} %bitcast.7), calls=%async_computation | async-start | bytes 2097152 | tf_op jit(solution)/shard_map/all_to_all | solution.py:138
  24.0 10.0 %copy-start.26 = (s32[16]{0:T(128)S(1)}, s32[16]{0:T(128)}, u32[]{:S(2)}) copy-start(s32[16]{0:T(128)} %param.12) | copy-start | bytes 196
  38.7 5.7 %copy-start.14 = (f32[16,8]{1,0:T(8,128)}, f32[16,8]{1,0:T(8,128)S(1)}, u32[]{:S(2)}) copy-start(f32[16,8]{1,0:T(8,128)S(1)} %get-tuple-element.63) | copy-start | bytes 1540
  41.0 3.4 %copy-start.16 = (f32[16,8]{1,0:T(8,128)}, f32[16,8]{1,0:T(8,128)S(1)}, u32[]{:S(2)}) copy-start(f32[16,8]{1,0:T(8,128)S(1)} %get-tuple-element.65) | copy-start | bytes 1540
  41.0 6.8 %copy-start.7 = (f32[16,8,512]{2,1,0:T(8,128)}, f32[16,8,512]{2,1,0:T(8,128)S(1)}, u32[]{:S(2)}) copy-start(f32[16,8,512]{2,1,0:T(8,128)S(1)} %get-tuple-element.66) | copy-start | bytes 786436
  43.5 4.4 %copy-start.9 = (f32[16,8,512]{2,1,0:T(8,128)}, f32[16,8,512]{2,1,0:T(8,128)S(1)}, u32[]{:S(2)}) copy-start(f32[16,8,512]{2,1,0:T(8,128)S(1)} %get-tuple-element.68) | copy-start | bytes 786436
  43.5 4.9 %copy-start.6 = (bf16[1024,512]{1,0:T(8,128)(2,1)S(1)}, bf16[1024,512]{1,0:T(8,128)(2,1)}, u32[]{:S(2)}) copy-start(bf16[1024,512]{1,0:T(8,128)(2,1)} %param.14) | copy-start | bytes 3145732
  55.0 7.9 %copy-start.4 = (f32[1024,1024]{1,0:T(8,128)}, f32[1024,1024]{1,0:T(8,128)S(1)}, u32[]{:S(2)}) copy-start(f32[1024,1024]{1,0:T(8,128)S(1)} %get-tuple-element.59) | copy-start | bytes 12582916
  56.0 7.0 %copy-start.3 = (f32[1024,1024]{1,0:T(8,128)S(1)}, f32[1024,1024]{1,0:T(8,128)}, u32[]{:S(2)}) copy-start(f32[1024,1024]{1,0:T(8,128)} %fusion.130) | copy-start | bytes 12582916
  62.9 5.2 %copy-start.5 = (f32[1024,1024]{1,0:T(8,128)}, f32[1024,1024]{1,0:T(8,128)S(1)}, u32[]{:S(2)}) copy-start(f32[1024,1024]{1,0:T(8,128)S(1)} %get-tuple-element.60) | copy-start | bytes 12582916
  62.9 5.3 %copy-start.27 = (bf16[1024,512]{1,0:T(8,128)(2,1)S(1)}, bf16[1024,512]{1,0:T(8,128)(2,1)}, u32[]{:S(2)}) copy-start(bf16[1024,512]{1,0:T(8,128)(2,1)} %param.15) | copy-start | bytes 3145732
  81.7 6.8 %copy-start.10 = (f32[16,8,512]{2,1,0:T(8,128)S(1)}, f32[16,8,512]{2,1,0:T(8,128)}, u32[]{:S(2)}) copy-start(f32[16,8,512]{2,1,0:T(8,128)} %copy-done.9) | copy-start | bytes 786436
  81.7 6.8 %copy-start.21 = (f32[16,8]{1,0:T(8,128)S(1)}, f32[16,8]{1,0:T(8,128)}, u32[]{:S(2)}) copy-start(f32[16,8]{1,0:T(8,128)} %copy-done.20) | copy-start | bytes 1540
  81.7 6.8 %copy-start.24 = (f32[16,8]{1,0:T(8,128)S(1)}, f32[16,8]{1,0:T(8,128)}, u32[]{:S(2)}) copy-start(f32[16,8]{1,0:T(8,128)} %get-tuple-element.71) | copy-start | bytes 1540
  83.3 7.4 %copy-start.13 = (f32[16,8,128]{2,1,0:T(8,128)S(1)}, f32[16,8,128]{2,1,0:T(8,128)}, u32[]{:S(2)}) copy-start(f32[16,8,128]{2,1,0:T(8,128)} %fusion.103) | copy-start | bytes 196612
  83.3 7.4 %copy-start.15 = (f32[16,8]{1,0:T(8,128)S(1)}, f32[16,8]{1,0:T(8,128)}, u32[]{:S(2)}) copy-start(f32[16,8]{1,0:T(8,128)} %copy-done.14) | copy-start | bytes 1540
  83.3 7.5 %copy-start.17 = (f32[16,8]{1,0:T(8,128)S(1)}, f32[16,8]{1,0:T(8,128)}, u32[]{:S(2)}) copy-start(f32[16,8]{1,0:T(8,128)} %copy-done.16) | copy-start | bytes 1540
  83.3 7.5 %copy-start.18 = (f32[16,8]{1,0:T(8,128)S(1)}, f32[16,8]{1,0:T(8,128)}, u32[]{:S(2)}) copy-start(f32[16,8]{1,0:T(8,128)} %get-tuple-element.12) | copy-start | bytes 1540
  83.3 7.5 %copy-start.19 = (f32[16,8]{1,0:T(8,128)S(1)}, f32[16,8]{1,0:T(8,128)}, u32[]{:S(2)}) copy-start(f32[16,8]{1,0:T(8,128)} %get-tuple-element.13) | copy-start | bytes 1540
  83.3 7.5 %copy-start.8 = (f32[16,8,512]{2,1,0:T(8,128)S(1)}, f32[16,8,512]{2,1,0:T(8,128)}, u32[]{:S(2)}) copy-start(f32[16,8,512]{2,1,0:T(8,128)} %copy-done.7) | copy-start | bytes 786436
  83.3 56.5 %all-to-all-start.1 = ((f32[8,16,4096]{2,1,0:T(8,128)}), f32[8,16,4096]{2,1,0:T(8,128)S(1)}, u32[]{:S(2)}, u32[]{:S(2)}) async-start(f32[8,16,4096]{2,1,0:T(8,128)} %pad_maximum_fusion), calls=%async_computation.1 | async-start | bytes 4194304 | tf_op jit(solution)/shard_map/all_to_all | solution.py:162
  90.6 5.5 %copy-start.12 = (pred[8,2,8,16]{3,2,1,0:T(8,128)(4,1)S(1)}, pred[8,2,8,16]{3,2,1,0:T(8,128)(4,1)}, u32[]{:S(2)}) copy-start(pred[8,2,8,16]{3,2,1,0:T(8,128)(4,1)} %copy-done.11) | copy-start | bytes 6148
  90.6 5.6 %copy-start.23 = (f32[16,8]{1,0:T(8,128)S(1)}, f32[16,8]{1,0:T(8,128)}, u32[]{:S(2)}) copy-start(f32[16,8]{1,0:T(8,128)} %get-tuple-element.44) | copy-start | bytes 1540
  90.6 5.7 %copy-start.22 = (f32[16,8]{1,0:T(8,128)S(1)}, f32[16,8]{1,0:T(8,128)}, u32[]{:S(2)}) copy-start(f32[16,8]{1,0:T(8,128)} %get-tuple-element.72) | copy-start | bytes 1540
  95.5 5.4 %collective-permute-start = (f32[1,16,32]{2,1,0:T(8,128)S(1)}, f32[1,16,32]{2,1,0:T(8,128)S(1)}, u32[]{:S(2)}, u32[]{:S(2)}) collective-permute-start(f32[1,16,32]{2,1,0:T(8,128)S(1)} %get-tuple-element.36), channel_id=1, source_target_pairs={{0,2},{2,0},{4,6},{6,4},{8,10},{10,8},{12,14},{14,12},{1,3},{3,1},... | collective-permute-start | bytes 6152 | tf_op jit(solution)/shard_map/ppermute | solution.py:28
  96.1 48.0 %copy-start.1 = (s32[128,1]{0,1:T(1,128)S(1)}, s32[128,1]{0,1:T(1,128)}, u32[]{:S(2)}) copy-start(s32[128,1]{0,1:T(1,128)} %param.10) | copy-start | bytes 1540
  96.6 27.2 %collective-permute-start.1 = (f32[1,16,32]{2,1,0:T(8,128)S(1)}, f32[1,16,32]{2,1,0:T(8,128)S(1)}, u32[]{:S(2)}, u32[]{:S(2)}) collective-permute-start(f32[1,16,32]{2,1,0:T(8,128)S(1)} %get-tuple-element.35), channel_id=1, source_target_pairs={{0,4},{2,6},{4,0},{6,2},{8,12},{10,14},{12,8},{14,10},{1,5},{3,7},... | collective-permute-start | bytes 6152 | tf_op jit(solution)/shard_map/ppermute | solution.py:28
  98.2 28.0 %collective-permute-start.2 = (f32[1,16,32]{2,1,0:T(8,128)S(1)}, f32[1,16,32]{2,1,0:T(8,128)S(1)}, u32[]{:S(2)}, u32[]{:S(2)}) collective-permute-start(f32[1,16,32]{2,1,0:T(8,128)S(1)} %get-tuple-element.34), channel_id=1, source_target_pairs={{0,6},{2,4},{4,2},{6,0},{8,14},{10,12},{12,10},{14,8},{1,7},{3,5},... | collective-permute-start | bytes 6152 | tf_op jit(solution)/shard_map/ppermute | solution.py:28
  98.2 40.5 %collective-permute-start.3 = (f32[1,16,32]{2,1,0:T(8,128)S(1)}, f32[1,16,32]{2,1,0:T(8,128)S(1)}, u32[]{:S(2)}, u32[]{:S(2)}) collective-permute-start(f32[1,16,32]{2,1,0:T(8,128)S(1)} %get-tuple-element.33), channel_id=1, source_target_pairs={{0,8},{2,10},{4,12},{6,14},{8,0},{10,2},{12,4},{14,6},{1,9},{3,11}... | collective-permute-start | bytes 6152 | tf_op jit(solution)/shard_map/ppermute | solution.py:28
  100.8 37.9 %collective-permute-start.4 = (f32[1,16,32]{2,1,0:T(8,128)S(1)}, f32[1,16,32]{2,1,0:T(8,128)S(1)}, u32[]{:S(2)}, u32[]{:S(2)}) collective-permute-start(f32[1,16,32]{2,1,0:T(8,128)S(1)} %get-tuple-element.32), channel_id=1, source_target_pairs={{0,10},{2,8},{4,14},{6,12},{8,2},{10,0},{12,6},{14,4},{1,11},{3,9}... | collective-permute-start | bytes 6152 | tf_op jit(solution)/shard_map/ppermute | solution.py:28
  101.0 37.8 %collective-permute-start.5 = (f32[1,16,32]{2,1,0:T(8,128)S(1)}, f32[1,16,32]{2,1,0:T(8,128)S(1)}, u32[]{:S(2)}, u32[]{:S(2)}) collective-permute-start(f32[1,16,32]{2,1,0:T(8,128)S(1)} %get-tuple-element.31), channel_id=1, source_target_pairs={{0,12},{2,14},{4,8},{6,10},{8,4},{10,6},{12,0},{14,2},{1,13},{3,15... | collective-permute-start | bytes 6152 | tf_op jit(solution)/shard_map/ppermute | solution.py:28
  123.8 15.0 %collective-permute-start.6 = (f32[1,16,32]{2,1,0:T(8,128)S(1)}, f32[1,16,32]{2,1,0:T(8,128)S(1)}, u32[]{:S(2)}, u32[]{:S(2)}) collective-permute-start(f32[1,16,32]{2,1,0:T(8,128)S(1)} %get-tuple-element.30), channel_id=1, source_target_pairs={{0,14},{2,12},{4,10},{6,8},{8,6},{10,4},{12,2},{14,0},{1,15},{3,13... | collective-permute-start | bytes 6152 | tf_op jit(solution)/shard_map/ppermute | solution.py:28
  (5 other events, 8.5 us)
